TPU v7x, 32 devices: a whole 2x2x4 slice. The times are simulated.
32 devices in a mesh: scen: 4 (over x, core), var: 8 (over z, y).
Axes of the slice: x: 2, y: 2, z: 4, core: 2. Of those that a mesh axis runs over, the one named last changes fastest.
Arguments:
- start_point: float32 [512, 65536], P('scen', 'var'), may hold values from -1 to 1
- multipliers: float32 [512, 65536], P('scen', 'var'), may hold values from -3 to 3
- cost: bfloat16 [512, 65536], P('scen', 'var'), may hold values from -6 to 6
- curvature: bfloat16 [512, 65536], P('scen', 'var'), may hold values from 0.5 to 2
- recourse_rhs: float32 [512, 512], P('scen'), may hold values from -12 to 12
- technology: bfloat16 [512, 65536], P(None, 'var'), may hold values from -0.0234375 to 0.0234375
- scenario_weight: float32 [512], P('scen'), may hold values from 1 to 30
- previous_mean: float32 [4, 65536], P(None, 'var'), may hold values from -1 to 1
- active: int32 [512, 512], P('scen', 'var'), may hold values 0 or 1
Outputs:
- iterate: float32 [512, 65536], P('scen', 'var')
- new_multipliers: float32 [512, 65536], P('scen', 'var')
- bundle_mean: float32 [4, 65536], P(None, 'var')
- primal_norm: float32 [], replicated
- dual_norm: float32 [], replicated
All inputs are finite; a program needn't handle non-finite values. No bound on the sum of `active` on one device may be relied on, other than what follows from the above.
Results may differ from a plain program's by a relative error of at most 0.0007.
Values sent between devices are 32-bit elements; how exact they have to be, the bound alone decides.
A program may use at most 64 MiB of HBM per device.

v0:
```python
import jax
import jax.numpy as jnp
from jax import lax
from jax.sharding import PartitionSpec as P

V = 65536
BLK = 128
STEPS = 8


highest = lax.Precision.HIGHEST
penalty = 1.0
recourse_scale = 4.0
stride = 0.2
epsilon = 1e-06


def from_partner(block, axis, bit):
    count = lax.axis_size(axis)
    route = []
    for low in range(count):
        high = low | 1 << bit
        if high != low and high < count:
            route += [(low, high), (high, low)]
    return lax.ppermute(block, axis, route)


def shards(
    start_point,
    multipliers,
    cost,
    curvature,
    recourse_rhs,
    technology,
    scenario_weight,
    previous_mean,
    active,
):
    scen_rows, var_cols = start_point.shape
    groups = previous_mean.shape[0]
    group_size = lax.axis_size("scen") // groups
    position = lax.axis_index("scen")
    my_node = position // group_size
    node_of = jnp.full((scen_rows,), my_node, jnp.int32)
    member = (node_of[:, None] == jnp.arange(groups, dtype=jnp.int32)[None, :]).astype(jnp.float32)
    bundle_mass = lax.psum(jnp.sum(member * scenario_weight[:, None], axis=0), "scen")
    anchor = jnp.dot(member, previous_mean, precision=highest, preferred_element_type=jnp.float32)
    linear = cost.astype(jnp.float32) + multipliers - penalty * anchor
    diagonal = curvature.astype(jnp.float32) + penalty
    active_mask = (active > 0)[:, :, None]
    iterate = start_point
    for sweep in range(STEPS):
        rounded = iterate.astype(jnp.bfloat16)
        partial_image = lax.dot_general(
            rounded, technology, (((1,), (1,)), ((), ())), preferred_element_type=jnp.float32
        )
        image = lax.psum(partial_image, "var")
        shortfall = (image - recourse_rhs).astype(jnp.bfloat16)
        pullback = jnp.dot(shortfall, technology, preferred_element_type=jnp.float32)
        stepped = jnp.clip(
            iterate - stride * (diagonal * iterate + linear + recourse_scale * pullback), -1.0, 1.0
        )
        blocked = jnp.where(
            active_mask, stepped.reshape(scen_rows, -1, BLK), iterate.reshape(scen_rows, -1, BLK)
        )
        iterate = blocked.reshape(scen_rows, var_cols)
    weighted = scenario_weight[:, None] * iterate
    normaliser = jnp.sum(bundle_mass) * V
    own_total = jnp.sum(weighted, axis=0, keepdims=True)
    for bit in range(group_size.bit_length() - 1):
        own_total = own_total + from_partner(own_total, "scen", bit)
    own_mass = jnp.sum(
        bundle_mass * (jnp.arange(groups, dtype=jnp.int32) == my_node).astype(jnp.float32)
    )
    mean_row = own_total / own_mass
    old_row = lax.dynamic_slice_in_dim(previous_mean, my_node, 1, 0)
    leader = (position % group_size == 0).astype(jnp.float32)
    centred = iterate - mean_row
    drift_part = leader * own_mass * jnp.sum((mean_row - old_row) ** 2)
    spread_part = jnp.sum(scenario_weight[:, None] * centred * centred)
    drift_sum, spread = lax.psum((drift_part, spread_part), ("scen", "var"))
    collected = lax.all_gather(mean_row, "scen", axis=0, tiled=True)
    bundle_mean = collected.reshape(groups, group_size, var_cols)[:, 0, :]
    primal_norm = jnp.sqrt(spread / normaliser + epsilon)
    dual_norm = penalty * jnp.sqrt(drift_sum / normaliser + epsilon)
    factor = penalty * jnp.sqrt(primal_norm / dual_norm)
    new_multipliers = multipliers + factor * centred
    return (iterate, new_multipliers, bundle_mean, primal_norm, dual_norm)


def solution(mesh):
    placed = (
        P("scen", "var"),
        P("scen", "var"),
        P("scen", "var"),
        P("scen", "var"),
        P("scen", None),
        P(None, "var"),
        P("scen"),
        P(None, "var"),
        P("scen", "var"),
    )
    return jax.shard_map(
        shards,
        mesh=mesh,
        in_specs=placed,
        out_specs=(P("scen", "var"), P("scen", "var"), P(None, "var"), P(), P()),
        check_vma=False,
    )
```

profile of v0, /device:TPU:0, one launch (start us, length us, event | category | flops | bytes accessed | tf_op | source)
XLA Modules:
  0.0 789.0 jit_solution(14389353718733308539)
XLA Ops:
  7.2 8.3 %fusion.55 = f32[128,512]{1,0:T(8,128)} fusion(bf16[512,8192]{1,0:T(8,128)(2,1)} %param.14, f32[128,8192]{1,0:T(8,128)} %param.9), kind=kOutput, calls=%fused_computation.68 | convolution fusion | flops 1074790400 | bytes 12845056 | tf_op jit(solution)/shard_map/dot_general | solution.py:54
  15.7 0.1 copy.16
  15.8 6.9 convolution_subtract_fusion
  22.8 66.7 %all-reduce.10.cloned.1.call-done = f32[128,512]{1,0:T(8,128)} async-done(((f32[128,512]{1,0:T(8,128)}), f32[128,512]{1,0:T(8,128)}) %all-reduce.10.cloned.1.call-update) | async-done | bytes 262160 | tf_op jit(solution)/shard_map/psum | solution.py:57
  89.4 2.7 broadcast_in_dim.37
  92.2 9.2 %fusion.39 = f32[128,8192]{1,0:T(8,128)S(1)} fusion(f32[128,8192]{1,0:T(8,128)} %param.9, bf16[512,8192]{1,0:T(8,128)(2,1)} %param.14, f32[128,8192]{1,0:T(8,128)} %convolution_subtract_fusion, bf16[128,8192]{1,0:T(8,128)(2,1)S(1)} %copy-done, f32[128,512]{1,0:T(8,128)} %all-reduce.10.cloned.1.call-done, f32[128,512]{1,0:T(8,128)S(1)} %copy-done.8, ...), kind=kOutput, calls=%fused_computation.48 | convolution fusion | flops 1084358656 | bytes 24641536 | tf_op jit(solution)/shard_map/dot_general | solution.py:59
  101.4 2.0 copy-done.7
  103.4 3.6 fusion.53
  107.1 0.5 all-reduce.14.cloned.1.call-start
  107.6 69.9 %all-reduce.12.cloned.1.call-done = f32[128,512]{1,0:T(8,128)} async-done(((f32[128,512]{1,0:T(8,128)}), f32[128,512]{1,0:T(8,128)}) %all-reduce.12.cloned.1.call-update) | async-done | bytes 262160 | tf_op jit(solution)/shard_map/psum | solution.py:57
  177.5 9.0 %fusion.37 = f32[128,8192]{1,0:T(8,128)S(1)} fusion(f32[128,8192]{1,0:T(8,128)} %copy-done.7, bf16[512,8192]{1,0:T(8,128)(2,1)} %param.14, f32[128,8192]{1,0:T(8,128)} %convolution_subtract_fusion, bf16[128,8192]{1,0:T(8,128)(2,1)S(1)} %copy-done, f32[128,512]{1,0:T(8,128)} %all-reduce.12.cloned.1.call-done, f32[128,512]{1,0:T(8,128)S(1)} %copy-done.8, ...), kind=kOutput, calls=%fused_computation.46 | convolution fusion | flops 1084358656 | bytes 24641536 | tf_op jit(solution)/shard_map/dot_general | solution.py:59
  186.5 2.0 copy-done.2
  188.5 7.0 fusion.51
  195.6 0.0 all-reduce.16.cloned.1.call-start
  195.6 70.3 %all-reduce.14.cloned.1.call-done = f32[128,512]{1,0:T(8,128)} async-done(((f32[128,512]{1,0:T(8,128)}), f32[128,512]{1,0:T(8,128)}) %all-reduce.14.cloned.1.call-update) | async-done | bytes 262160 | tf_op jit(solution)/shard_map/psum | solution.py:57
  265.9 9.0 %fusion.35 = f32[128,8192]{1,0:T(8,128)S(1)} fusion(f32[128,8192]{1,0:T(8,128)} %copy-done.2, bf16[512,8192]{1,0:T(8,128)(2,1)} %param.14, f32[128,8192]{1,0:T(8,128)} %convolution_subtract_fusion, bf16[128,8192]{1,0:T(8,128)(2,1)S(1)} %copy-done, f32[128,512]{1,0:T(8,128)} %all-reduce.14.cloned.1.call-done, f32[128,512]{1,0:T(8,128)S(1)} %copy-done.8, ...), kind=kOutput, calls=%fused_computation.44 | convolution fusion | flops 1084358656 | bytes 24641536 | tf_op jit(solution)/shard_map/dot_general | solution.py:59
  275.0 2.0 copy-done.3
  277.0 7.0 fusion.49
  284.0 0.2 all-reduce.18.cloned.1.call-start
  284.2 70.2 %all-reduce.16.cloned.1.call-done = f32[128,512]{1,0:T(8,128)} async-done(((f32[128,512]{1,0:T(8,128)}), f32[128,512]{1,0:T(8,128)}) %all-reduce.16.cloned.1.call-update) | async-done | bytes 262160 | tf_op jit(solution)/shard_map/psum | solution.py:57
  354.4 9.0 %fusion.33 = f32[128,8192]{1,0:T(8,128)S(1)} fusion(f32[128,8192]{1,0:T(8,128)} %copy-done.3, bf16[512,8192]{1,0:T(8,128)(2,1)} %param.14, f32[128,8192]{1,0:T(8,128)} %convolution_subtract_fusion, bf16[128,8192]{1,0:T(8,128)(2,1)S(1)} %copy-done, f32[128,512]{1,0:T(8,128)} %all-reduce.16.cloned.1.call-done, f32[128,512]{1,0:T(8,128)S(1)} %copy-done.8, ...), kind=kOutput, calls=%fused_computation.42 | convolution fusion | flops 1084358656 | bytes 24641536 | tf_op jit(solution)/shard_map/dot_general | solution.py:59
  363.4 2.0 copy-done.4
  365.4 7.0 fusion.47
  372.5 70.4 %all-reduce.18.cloned.1.call-done = f32[128,512]{1,0:T(8,128)} async-done(((f32[128,512]{1,0:T(8,128)}), f32[128,512]{1,0:T(8,128)}) %all-reduce.18.cloned.1.call-update) | async-done | bytes 262160 | tf_op jit(solution)/shard_map/psum | solution.py:57
  442.9 9.0 %fusion.31 = f32[128,8192]{1,0:T(8,128)S(1)} fusion(f32[128,8192]{1,0:T(8,128)} %copy-done.4, bf16[512,8192]{1,0:T(8,128)(2,1)} %param.14, f32[128,8192]{1,0:T(8,128)} %convolution_subtract_fusion, bf16[128,8192]{1,0:T(8,128)(2,1)S(1)} %copy-done, f32[128,512]{1,0:T(8,128)} %all-reduce.18.cloned.1.call-done, f32[128,512]{1,0:T(8,128)S(1)} %copy-done.8, ...), kind=kOutput, calls=%fused_computation.40 | convolution fusion | flops 1084358656 | bytes 24641536 | tf_op jit(solution)/shard_map/dot_general | solution.py:59
  451.9 2.0 copy-done.5
  453.9 7.0 fusion.45
  461.0 0.3 all-reduce.22.cloned.1.call-start
  461.2 70.1 %all-reduce.20.cloned.1.call-done = f32[128,512]{1,0:T(8,128)} async-done(((f32[128,512]{1,0:T(8,128)}), f32[128,512]{1,0:T(8,128)}) %all-reduce.20.cloned.1.call-update) | async-done | bytes 262160 | tf_op jit(solution)/shard_map/psum | solution.py:57
  531.4 9.0 %fusion.29 = f32[128,8192]{1,0:T(8,128)S(1)} fusion(f32[128,8192]{1,0:T(8,128)} %copy-done.5, bf16[512,8192]{1,0:T(8,128)(2,1)} %param.14, f32[128,8192]{1,0:T(8,128)} %convolution_subtract_fusion, bf16[128,8192]{1,0:T(8,128)(2,1)S(1)} %copy-done, f32[128,512]{1,0:T(8,128)} %all-reduce.20.cloned.1.call-done, f32[128,512]{1,0:T(8,128)S(1)} %copy-done.8, ...), kind=kOutput, calls=%fused_computation.38 | convolution fusion | flops 1084358656 | bytes 24641536 | tf_op jit(solution)/shard_map/dot_general | solution.py:59
  540.4 2.0 copy-done.6
  542.4 7.0 fusion.43
  549.5 70.3 %all-reduce.22.cloned.1.call-done = f32[128,512]{1,0:T(8,128)} async-done(((f32[128,512]{1,0:T(8,128)}), f32[128,512]{1,0:T(8,128)}) %all-reduce.22.cloned.1.call-update) | async-done | bytes 262160 | tf_op jit(solution)/shard_map/psum | solution.py:57
  619.8 9.0 %fusion.27 = f32[128,8192]{1,0:T(8,128)S(1)} fusion(f32[128,8192]{1,0:T(8,128)} %copy-done.6, bf16[512,8192]{1,0:T(8,128)(2,1)} %param.14, f32[128,8192]{1,0:T(8,128)} %convolution_subtract_fusion, bf16[128,8192]{1,0:T(8,128)(2,1)S(1)} %copy-done, f32[128,512]{1,0:T(8,128)} %all-reduce.22.cloned.1.call-done, f32[128,512]{1,0:T(8,128)S(1)} %copy-done.8, ...), kind=kOutput, calls=%fused_computation.36 | convolution fusion | flops 1084358656 | bytes 24641536 | tf_op jit(solution)/shard_map/dot_general | solution.py:59
  628.8 2.0 copy-done.1
  630.8 7.0 fusion.41
  637.9 0.2 multiply_reduce_fusion.2
  638.1 5.9 psum.85
  644.0 0.6 fusion.60
  645.3 63.0 %all-reduce.24.cloned.1.call-done = f32[128,512]{1,0:T(8,128)} async-done(((f32[128,512]{1,0:T(8,128)}), f32[128,512]{1,0:T(8,128)}) %all-reduce.24.cloned.1.call-update) | async-done | bytes 262160 | tf_op jit(solution)/shard_map/psum | solution.py:57
  708.3 11.2 %multiply_reduce_fusion = (f32[8192]{0:T(1024)S(1)}, f32[128,8192]{1,0:T(8,128)}) fusion(f32[128]{0:T(128)S(1)} %copy-done.11, f32[128,8192]{1,0:T(8,128)} %copy-done.1, bf16[512,8192]{1,0:T(8,128)(2,1)} %param.14, f32[128,512]{1,0:T(8,128)} %all-reduce.24.cloned.1.call-done, f32[128,512]{1,0:T(8,128)S(1)} %copy-done.8, ...), kind=kOutput, calls=%fused_computation.52 | convolution fusion | flops 1086447616 | bytes 24674816 | tf_op jit(solution)/shard_map/dot_general | solution.py:59
  719.5 0.7 broadcast_divide_fusion
  720.2 0.7 multiply_reduce_fusion.1
  722.1 3.9 fusion.40
  726.1 5.4 all-gather
  731.5 39.7 %all-reduce = (f32[]{:T(128)}, f32[]{:T(128)}) all-reduce(f32[]{:T(128)} %fusion.40, f32[]{:T(128)S(6)} %mul.145), channel_id=1, replica_groups=mesh['scen'=4,'var'=8] {'scen','var'}, use_global_device_ids=true, to_apply=%region_13.14 | all-reduce | flops 2 | bytes 16 | tf_op jit(solution)/shard_map/psum | solution.py:81
  772.7 6.1 multiply_add_fusion
  778.8 0.7 reshape.75
  (37 shorter events, 0.4 us)
Async XLA Ops:
  7.2 8.5 %copy-start.10 = (s32[128,64]{0,1:T(8,128)S(1)}, s32[128,64]{0,1:T(8,128)}, u32[]{:S(2)}) copy-start(s32[128,64]{0,1:T(8,128)} %param.17) | copy-start | bytes 98308
  7.2 8.6 %copy-start.9 = (f32[4,8192]{1,0:T(4,128)S(1)}, f32[4,8192]{1,0:T(4,128)}, u32[]{:S(2)}) copy-start(f32[4,8192]{1,0:T(4,128)} %param.16) | copy-start | bytes 393220
  7.2 82.3 %all-reduce.10.cloned.1.call-start = ((), (), s32[]{:S(2)}) async-start(), calls=%async_computation | async-start | bytes 524288 | tf_op jit(solution)/shard_map/psum | solution.py:57
  15.6 161.9 %all-reduce.12.cloned.1.call-start = ((), (), s32[]{:S(2)}) async-start(), calls=%async_computation.1 | async-start | bytes 524288 | tf_op jit(solution)/shard_map/psum | solution.py:57
  15.8 76.4 %copy-start = (bf16[128,8192]{1,0:T(8,128)(2,1)S(1)}, bf16[128,8192]{1,0:T(8,128)(2,1)}, u32[]{:S(2)}) copy-start(bf16[128,8192]{1,0:T(8,128)(2,1)} %param.12) | copy-start | bytes 6291460
  15.8 76.4 %copy-start.8 = (f32[128,512]{1,0:T(8,128)S(1)}, f32[128,512]{1,0:T(8,128)}, u32[]{:S(2)}) copy-start(f32[128,512]{1,0:T(8,128)} %param.13) | copy-start | bytes 786436
  89.4 14.0 %slice-start = ((s8[8388608]{0:T(1024)(128)(4,1)}), s8[4194304]{0:T(1024)(128)(4,1)S(1)}, s32[]{:S(2)}) async-start(s8[8388608]{0:T(1024)(128)(4,1)} %bitcast.28), calls=%async_computation.8 | async-start | bytes 8388608
  92.2 11.2 %slice-start.1 = ((s8[8388608]{0:T(1024)(128)(4,1)}), s8[4194304]{0:T(1024)(128)(4,1)S(1)}, s32[]{:S(2)}) async-start(s8[8388608]{0:T(1024)(128)(4,1)} %bitcast.28), calls=%async_computation.9 | async-start | bytes 8388608
  101.4 2.0 copy-start.7
  107.1 158.9 %all-reduce.14.cloned.1.call-start = ((), (), s32[]{:S(2)}) async-start(), calls=%async_computation.2 | async-start | bytes 524288 | tf_op jit(solution)/shard_map/psum | solution.py:57
  186.5 2.0 copy-start.2
  195.6 158.8 %all-reduce.16.cloned.1.call-start = ((), (), s32[]{:S(2)}) async-start(), calls=%async_computation.3 | async-start | bytes 524288 | tf_op jit(solution)/shard_map/psum | solution.py:57
  275.0 2.0 copy-start.3
  284.0 158.9 %all-reduce.18.cloned.1.call-start = ((), (), s32[]{:S(2)}) async-start(), calls=%async_computation.4 | async-start | bytes 524288 | tf_op jit(solution)/shard_map/psum | solution.py:57
  363.4 2.0 copy-start.4
  372.5 158.9 %all-reduce.20.cloned.1.call-start = ((), (), s32[]{:S(2)}) async-start(), calls=%async_computation.5 | async-start | bytes 524288 | tf_op jit(solution)/shard_map/psum | solution.py:57
  451.9 2.0 copy-start.5
  461.0 158.8 %all-reduce.22.cloned.1.call-start = ((), (), s32[]{:S(2)}) async-start(), calls=%async_computation.6 | async-start | bytes 524288 | tf_op jit(solution)/shard_map/psum | solution.py:57
  540.4 2.0 copy-start.6
  549.4 158.8 %all-reduce.24.cloned.1.call-start = ((), (), s32[]{:S(2)}) async-start(), calls=%async_computation.7 | async-start | bytes 524288 | tf_op jit(solution)/shard_map/psum | solution.py:57
  628.8 2.0 copy-start.1
  630.8 7.1 copy-start.11
Sparse Core Ops, SparseCore 0:
  15.7 73.7 all-reduce.9
  107.2 70.2 all-reduce.11
  195.7 70.1 all-reduce.13
  284.1 70.2 all-reduce.15
  372.6 70.2 all-reduce.17
  461.1 70.2 all-reduce.19
  549.6 70.1 all-reduce.21
  638.0 70.2 all-reduce.23
where the time goes:
time: 796 us; the launch traced here: 789 us
  waiting for transfers between devices  551 us (69%)
  matrix products  135 us (17%)
  blocking collectives  51 us (6%)
  between operations  20.5 us (3%)
  local copies, waits for them, and re-layouts  17.6 us (2%)
  other arithmetic  12.2 us (2%)
    psum x8, waiting for transfers between devices, shards(): image = lax.psum(partial_image, 'var')  551 us
    dot_general x8, matrix products, shards(): jnp.dot(shortfall, technology, preferred_element_type=jnp.float32)  74.5 us
    dot_general x8, matrix products, shards(): lax.dot_general(rounded, technology, (((1,), (1,)), ((), ())), preferred_...  54 us
    psum x1, blocking collectives, shards(): drift_sum, spread = lax.psum((drift_part, spread_part), ('scen', 'var'))  39.7 us
  transfers between devices with their start and end apart: 8, of which 8 were waited for; matrix products, arithmetic and copies ran while one was open for 1% of the time, Pallas kernels for 0%

commit v1 on v0

v1 whole, which is shorter than its diff:
```python
import functools

import jax
import jax.numpy as jnp
from jax import lax
from jax.experimental import pallas as pl
from jax.experimental.pallas import tpu as pltpu
from jax.sharding import PartitionSpec as P

BLK = 128
STEPS = 8
LANES = 128

penalty = 1.0
recourse_scale = 4.0
stride = 0.2
epsilon = 1e-06


def kernel(
    n, count, nodes, pieces, sets,
    start_hbm, mult_hbm, cost_hbm, curv_hbm, rhs_ref, tech_hbm, weight_ref, prev_ref, active_ref,
    iterate_hbm, new_mult_hbm, mean_ref, norms_ref,
    tech, it, mult, cost, curv, keep, push, gate, part, landed, full, short, own, totals, scal_var, scal_scen,
    load_sem, store_sem, rs_send, rs_recv, ag_send, ag_recv, t_send, t_recv, v_send, v_recv, s_send, s_recv,
):
    me = lax.axis_index("var")
    pos = lax.axis_index("scen")
    per_node = count // nodes
    my_node = pos // per_node
    rows, cols = it.shape
    width = cols // pieces
    height = rows // sets

    def load(which, src, dst, piece):
        where = (slice(None), pl.ds(piece * width, width))
        return pltpu.make_async_copy(src.at[where], dst.at[where], load_sem.at[which, piece])

    loads = ((start_hbm, it), (tech_hbm, tech), (mult_hbm, mult), (cost_hbm, cost), (curv_hbm, curv))
    for early in ((0, 1), (2, 3, 4)):
        for piece in range(pieces):
            for which in early:
                load(which, *loads[which], piece).start()

    barrier = pltpu.get_barrier_semaphore()
    for k in range(1, n):
        pl.semaphore_signal(barrier, inc=1, device_id={"var": lax.rem(me + k, n)})
    for k in range(1, count):
        pl.semaphore_signal(barrier, inc=1, device_id={"scen": lax.rem(pos + k, count)})
    pl.semaphore_wait(barrier, n + count - 2)

    def scatter(g, k):
        to = lax.rem(me + k, n)
        return pltpu.make_async_remote_copy(
            src_ref=part.at[g, to], dst_ref=landed.at[g, k - 1],
            send_sem=rs_send.at[g, k - 1], recv_sem=rs_recv.at[g, k - 1], device_id={"var": to},
        )

    def gather(g, k):
        return pltpu.make_async_remote_copy(
            src_ref=full.at[g, me], dst_ref=full.at[g, me],
            send_sem=ag_send.at[g, k - 1], recv_sem=ag_recv.at[g, k - 1],
            device_id={"var": lax.rem(me + k, n)},
        )

    def pick_row(ref):
        row = ref[0:1, :]
        for node in range(1, nodes):
            row = jnp.where(my_node == node, ref[node : node + 1, :], row)
        own[...] = row

    def image_of(g, where):
        rounded = it[pl.ds(g * height, height), where].astype(jnp.bfloat16)
        found = lax.dot_general(
            rounded, tech[:, where], (((1,), (1,)), ((), ())), preferred_element_type=jnp.float32
        )
        return found.reshape(part.shape[1:])

    def send_parts(g):
        for k in range(1, n):
            scatter(g, k).start()

    for piece in range(pieces):
        where = pl.ds(piece * width, width)
        for which in (0, 1):
            load(which, *loads[which], piece).wait()
        for g in range(sets):
            found = image_of(g, where)
            part[g] = found if piece == 0 else part[g] + found
    for g in range(sets):
        send_parts(g)

    pick_row(prev_ref)
    for piece in range(pieces):
        for which in (2, 3, 4):
            load(which, *loads[which], piece).wait()
        for block in range(piece * (width // BLK), (piece + 1) * (width // BLK)):
            where = pl.ds(block * BLK, BLK)
            on = jnp.broadcast_to((active_ref[:, block : block + 1] > 0).astype(jnp.float32), (rows, BLK))
            linear = cost[:, where].astype(jnp.float32) + mult[:, where] - penalty * own[:, where]
            diagonal = curv[:, where].astype(jnp.float32) + penalty
            keep[:, where] = 1.0 - stride * diagonal * on
            push[:, where] = stride * linear * on
            gate[:, where] = stride * recourse_scale * on

    def reduce_parts():
        for g in range(sets):
            for k in range(1, n):
                scatter(g, k).wait_recv()
            found = part[g, me]
            for k in range(1, n):
                found = found + landed[g, k - 1]
            full[g, me] = found
            for k in range(1, n):
                gather(g, k).start()
            for k in range(1, n):
                scatter(g, k).wait_send()

    def take_image(g):
        for k in range(1, n):
            gather(g, k).wait_recv()
        image = full[g].reshape(height, full.shape[-1])
        short[g] = (image - rhs_ref[pl.ds(g * height, height), :]).astype(jnp.bfloat16)
        for k in range(1, n):
            gather(g, k).wait_send()

    def move(g, where):
        mine = pl.ds(g * height, height)
        pullback = jnp.dot(short[g], tech[:, where], preferred_element_type=jnp.float32)
        stepped = keep[mine, where] * it[mine, where] - push[mine, where] - gate[mine, where] * pullback
        new = jnp.clip(stepped, -1.0, 1.0)
        it[mine, where] = new
        return new

    def sweep(step, carry):
        reduce_parts()
        for g in range(sets):
            take_image(g)
            part[g] = jnp.zeros(part.shape[1:], jnp.float32)

            def one(piece, carry):
                where = pl.ds(pl.multiple_of(piece * width, width), width)
                move(g, where)
                part[g] = part[g] + image_of(g, where)
                return carry

            lax.fori_loop(0, pieces, one, 0)
            send_parts(g)
        return carry

    lax.fori_loop(0, STEPS - 1, sweep, 0)

    reduce_parts()
    weights = weight_ref[...]
    for g in range(sets):
        take_image(g)

        def last(piece, carry):
            where = pl.ds(pl.multiple_of(piece * width, width), width)
            new = move(g, where)
            total = jnp.sum(weights[g * height : (g + 1) * height] * new, axis=0, keepdims=True)
            totals[pos, :, where] = total if g == 0 else totals[pos, :, where] + total
            return carry

        lax.fori_loop(0, pieces, last, 0)
    totals[pos, :, pl.ds(cols, LANES)] = jnp.broadcast_to(jnp.sum(weights, axis=0, keepdims=True), (1, LANES))

    def share(ref, spot, axis, size, sends, recvs, k):
        return pltpu.make_async_remote_copy(
            src_ref=ref.at[spot], dst_ref=ref.at[spot], send_sem=sends.at[k - 1], recv_sem=recvs.at[k - 1],
            device_id={axis: lax.rem(spot + k, size)},
        )

    def spread_out(*what):
        for k in range(1, what[3]):
            share(*what, k).start()

    def collect(*what):
        for k in range(1, what[3]):
            share(*what, k).wait()

    exchange_t = (totals, pos, "scen", count, t_send, t_recv)
    spread_out(*exchange_t)
    out_it = pltpu.make_async_copy(it, iterate_hbm, store_sem.at[pieces])
    out_it.start()
    collect(*exchange_t)

    def mass_of(node):
        found = totals[node * per_node, :, pl.ds(cols, 1)]
        for p in range(node * per_node + 1, (node + 1) * per_node):
            found = found + totals[p, :, pl.ds(cols, 1)]
        return found

    masses = [mass_of(node) for node in range(nodes)]
    all_mass = masses[0]
    for mass in masses[1:]:
        all_mass = all_mass + mass

    drift = jnp.zeros((1, 1), jnp.float32)
    for node in range(nodes):
        total = totals[node * per_node, :, pl.ds(0, cols)]
        for p in range(node * per_node + 1, (node + 1) * per_node):
            total = total + totals[p, :, pl.ds(0, cols)]
        mean = total / masses[node]
        mean_ref[node : node + 1, :] = mean
        gap = mean - prev_ref[node : node + 1, :]
        drift = drift + masses[node] * jnp.sum(gap * gap, axis=1, keepdims=True)

    pick_row(mean_ref)

    def apart(piece):
        where = pl.ds(pl.multiple_of(piece * width, width), width)
        return where, it[:, where] - own[:, where]

    def widen(piece, carry):
        where, centred = apart(piece)
        return carry + jnp.sum(weights * centred * centred, axis=0, keepdims=True)

    spread = lax.fori_loop(0, pieces, widen, jnp.zeros((1, width), jnp.float32))
    spread = jnp.sum(spread, axis=1, keepdims=True)

    first_row = lax.broadcasted_iota(jnp.int32, scal_var.shape[1:], 0) == 0
    scal_var[me] = jnp.where(first_row, spread, drift)
    exchange_v = (scal_var, me, "var", n, v_send, v_recv)
    spread_out(*exchange_v)
    collect(*exchange_v)
    both = scal_var[0]
    for p in range(1, n):
        both = both + scal_var[p]
    scal_scen[pos] = both
    exchange_s = (scal_scen, pos, "scen", count, s_send, s_recv)
    spread_out(*exchange_s)
    collect(*exchange_s)
    both = scal_scen[0]
    drift = both[1:2, 0:1]
    for p in range(1, count):
        both = both + scal_scen[p]
    spread = both[0:1, 0:1]
    normaliser = all_mass * float(n * cols)
    primal = jnp.sqrt(spread / normaliser + epsilon)
    dual = penalty * jnp.sqrt(drift / normaliser + epsilon)
    factor = penalty * jnp.sqrt(primal / dual)
    norms_ref[...] = jnp.where(first_row, primal, dual)

    def store(piece):
        where = pl.ds(piece * width, width)
        return pltpu.make_async_copy(mult.at[:, where], new_mult_hbm.at[:, where], store_sem.at[piece])

    for piece in range(pieces):
        where, centred = apart(piece)
        mult[:, where] = mult[:, where] + factor * centred
        store(piece).start()
    for piece in range(pieces):
        store(piece).wait()
    out_it.wait()


def solution(mesh):
    n, count = mesh.shape["var"], mesh.shape["scen"]

    def shards(start, multipliers, cost, curvature, rhs, technology, weight, previous, active):
        rows, cols = start.shape
        m = technology.shape[0]
        nodes = previous.shape[0]
        sets = 2 if rows % (16 * n) == 0 else 1
        chunk = rows // sets // n
        pieces = 8
        f32 = jnp.float32
        dma = pltpu.SemaphoreType.DMA
        anywhere = pl.BlockSpec(memory_space=pl.ANY)
        vmem = pl.BlockSpec(memory_space=pltpu.VMEM)
        iterate, new_multipliers, mean, norms = pl.pallas_call(
            functools.partial(kernel, n, count, nodes, pieces, sets),
            out_shape=(
                jax.ShapeDtypeStruct((rows, cols), f32),
                jax.ShapeDtypeStruct((rows, cols), f32),
                jax.ShapeDtypeStruct((nodes, cols), f32),
                jax.ShapeDtypeStruct((8, LANES), f32),
            ),
            in_specs=[anywhere] * 4 + [vmem, anywhere, vmem, vmem, vmem],
            out_specs=(anywhere, anywhere, vmem, vmem),
            scratch_shapes=[
                pltpu.VMEM((m, cols), jnp.bfloat16),
                pltpu.VMEM((rows, cols), f32),
                pltpu.VMEM((rows, cols), f32),
                pltpu.VMEM((rows, cols), jnp.bfloat16),
                pltpu.VMEM((rows, cols), jnp.bfloat16),
                pltpu.VMEM((rows, cols), f32),
                pltpu.VMEM((rows, cols), f32),
                pltpu.VMEM((rows, cols), f32),
                pltpu.VMEM((sets, n, chunk, m), f32),
                pltpu.VMEM((sets, n - 1, chunk, m), f32),
                pltpu.VMEM((sets, n, chunk, m), f32),
                pltpu.VMEM((sets, rows // sets, m), jnp.bfloat16),
                pltpu.VMEM((1, cols), f32),
                pltpu.VMEM((count, 1, cols + LANES), f32),
                pltpu.VMEM((n, 8, LANES), f32),
                pltpu.VMEM((count, 8, LANES), f32),
                dma((5, pieces)),
                dma((pieces + 1,)),
                dma((sets, n - 1)),
                dma((sets, n - 1)),
                dma((sets, n - 1)),
                dma((sets, n - 1)),
                dma((count - 1,)),
                dma((count - 1,)),
                dma((n - 1,)),
                dma((n - 1,)),
                dma((count - 1,)),
                dma((count - 1,)),
            ],
            compiler_params=pltpu.CompilerParams(
                collective_id=0, has_side_effects=True, vmem_limit_bytes=60 * 1024 * 1024
            ),
        )(start, multipliers, cost, curvature, rhs, technology, weight.reshape(rows, 1), previous, active)
        return iterate, new_multipliers, mean, norms[0, 0], norms[1, 0]

    both = P("scen", "var")
    return jax.shard_map(
        shards,
        mesh=mesh,
        in_specs=(both, both, both, both, P("scen", None), P(None, "var"), P("scen"), P(None, "var"), both),
        out_specs=(both, both, P(None, "var"), P(), P()),
        check_vma=False,
    )
```

time: 796 us -> 173 us (0.22)
  waiting for transfers between devices: 551 us -> 0 us
  Pallas kernels: 0 us -> 160 us
  matrix products: 135 us -> 0 us
  blocking collectives: 51 us -> 0 us
  between operations: 20.5 us -> 0.64 us
  other arithmetic: 12.2 us -> 0 us
    psum x8 -> x0, waiting for transfers between devices: 551 us -> none  [shards(): image = lax.psum(partial_image, 'var')]
    pallas_call x0 -> x1, Pallas kernels: none -> 160 us  [shards(): pl.pallas_call(functools.partial(kernel, n, count, nodes, pieces, sets),...]
    dot_general x17 -> x0, matrix products: 135 us -> none  [the longest x8 74.5 us: shards(): jnp.dot(shortfall, technology, preferred_element_type=jnp.float32)]
    psum x2 -> x0, blocking collectives: 45.6 us -> none  [the longest x1 39.7 us: shards(): drift_sum, spread = lax.psum((drift_part, spread_part), ('scen', 'var'))]
  transfers between devices with their start and end apart: 8 -> 0, of which waited for: 8 -> 0; matrix products, arithmetic and copies ran while one was open for 1% -> 0% of each run, Pallas kernels for 0% -> 0%
where the time goes in v1:
time: 173 us; the launch traced here: 172 us
  Pallas kernels  160 us (92%)
  local copies, waits for them, and re-layouts  11.6 us (7%)
    pallas_call x1, Pallas kernels, shards(): pl.pallas_call(functools.partial(kernel, n, count, nodes, pieces, sets),...  160 us
    unnamed x8, local copies, waits for them, and re-layouts  8.92 us

profile of v1, /device:TPU:0, one launch (start us, length us, event | category | flops | bytes accessed | tf_op | source)
XLA Modules:
  0.0 172.3 jit_solution(14594210198619845267)
XLA Ops:
  0.6 1.4 copy.14.weight_ref
  2.0 1.5 copy.15.active_ref
  3.5 160.0 %shard_map.128 = (f32[128,8192]{1,0:T(8,128)}, f32[128,8192]{1,0:T(8,128)}, f32[4,8192]{1,0:T(4,128)}, f32[8,128]{1,0:T(8,128)}) custom-call(f32[128,8192]{1,0:T(8,128)} %start_hbm.1, f32[128,8192]{1,0:T(8,128)} %mult_hbm.1, bf16[128,8192]{1,0:T(8,128)(2,1)} %cost_hbm.1, bf16[128,8192]{1,0:T(8,128)(2,1)} %curv_hbm.1, f32[128,512]{1,0:T(8,128)} %rhs_ref.1, ...), custom_call_target="tpu_custom_call" | custom-call | tf_op jit(solution)/shard_map/pallas_call | solution.py:272
  163.5 1.3 fusion
  164.8 0.0 copy-start
  164.8 4.8 %copy.19 = f32[128,8192]{1,0:T(8,128)} copy(f32[128,8192]{1,0:T(8,128)} %get-tuple-element.20) | data formatting | bytes 8388608
  169.6 0.0 copy-done
  169.6 0.0 copy-start.1
  169.6 2.0 %copy.20 = f32[128,8192]{1,0:T(8,128)} copy(f32[128,8192]{1,0:T(8,128)S(1)} %copy-done) | data formatting | bytes 8388608
  171.6 0.0 copy-done.1
  171.6 0.7 copy.21
Async XLA Ops:
  164.8 4.8 %copy-start = (f32[128,8192]{1,0:T(8,128)S(1)}, f32[128,8192]{1,0:T(8,128)}, u32[]{:S(2)}) copy-start(f32[128,8192]{1,0:T(8,128)} %get-tuple-element.21) | copy-start | bytes 12582916
  169.6 2.0 %copy-start.1 = (f32[4,8192]{1,0:T(4,128)S(1)}, f32[4,8192]{1,0:T(4,128)}, u32[]{:S(2)}) copy-start(f32[4,8192]{1,0:T(4,128)} %get-tuple-element.22) | copy-start | bytes 393220

commit v2 on v1

--- a/solution.py
+++ b/solution.py
@@ -90,13 +90,14 @@
     for g in range(sets):
         send_parts(g)
 
+    active = jnp.transpose((active_ref[...] > 0).astype(jnp.float32))
     pick_row(prev_ref)
     for piece in range(pieces):
         for which in (2, 3, 4):
             load(which, *loads[which], piece).wait()
         for block in range(piece * (width // BLK), (piece + 1) * (width // BLK)):
             where = pl.ds(block * BLK, BLK)
-            on = jnp.broadcast_to((active_ref[:, block : block + 1] > 0).astype(jnp.float32), (rows, BLK))
+            on = jnp.broadcast_to(active[:, block : block + 1], (rows, BLK))
             linear = cost[:, where].astype(jnp.float32) + mult[:, where] - penalty * own[:, where]
             diagonal = curv[:, where].astype(jnp.float32) + penalty
             keep[:, where] = 1.0 - stride * diagonal * on
@@ -151,7 +152,7 @@
     lax.fori_loop(0, STEPS - 1, sweep, 0)
 
     reduce_parts()
-    weights = weight_ref[...]
+    weights = jnp.transpose(jnp.broadcast_to(weight_ref[...], (LANES, rows)))[:, 0:1]
     for g in range(sets):
         take_image(g)
 
@@ -312,7 +313,7 @@
             compiler_params=pltpu.CompilerParams(
                 collective_id=0, has_side_effects=True, vmem_limit_bytes=60 * 1024 * 1024
             ),
-        )(start, multipliers, cost, curvature, rhs, technology, weight.reshape(rows, 1), previous, active)
+        )(start, multipliers, cost, curvature, rhs, technology, weight.reshape(1, rows), previous, active.T)
         return iterate, new_multipliers, mean, norms[0, 0], norms[1, 0]
 
     both = P("scen", "var")

time: 173 us -> 170 us (0.983)
  local copies, waits for them, and re-layouts: 11.6 us -> 8.71 us
    unnamed x8 -> x7, local copies, waits for them, and re-layouts: 8.92 us -> 7.43 us
where the time goes in v2:
time: 170 us
  Pallas kernels  161 us (95%)
  local copies, waits for them, and re-layouts  8.71 us (5%)
    pallas_call x1, Pallas kernels, shards(): pl.pallas_call(functools.partial(kernel, n, count, nodes, pieces, sets),...  161 us
    unnamed x7, local copies, waits for them, and re-layouts  7.43 us

profile of v2, /device:TPU:0, one launch (start us, length us, event | category | flops | bytes accessed | tf_op | source)
XLA Modules:
  0.0 170.0 jit_solution(16898910844971167347)
XLA Ops:
  0.6 160.7 %shard_map.128 = (f32[128,8192]{1,0:T(8,128)}, f32[128,8192]{1,0:T(8,128)}, f32[4,8192]{1,0:T(4,128)}, f32[8,128]{1,0:T(8,128)}) custom-call(f32[128,8192]{1,0:T(8,128)} %start_hbm.1, f32[128,8192]{1,0:T(8,128)} %mult_hbm.1, bf16[128,8192]{1,0:T(8,128)(2,1)} %cost_hbm.1, bf16[128,8192]{1,0:T(8,128)(2,1)} %curv_hbm.1, f32[128,512]{1,0:T(8,128)} %rhs_ref.1, ...), custom_call_target="tpu_custom_call" | custom-call | tf_op jit(solution)/shard_map/pallas_call | solution.py:273
  161.3 1.3 fusion
  162.6 0.0 copy-start
  162.6 4.8 %copy.17 = f32[128,8192]{1,0:T(8,128)} copy(f32[128,8192]{1,0:T(8,128)} %get-tuple-element.20) | data formatting | bytes 8388608
  167.3 0.0 copy-done
  167.3 0.0 copy-start.1
  167.3 2.0 %copy.18 = f32[128,8192]{1,0:T(8,128)} copy(f32[128,8192]{1,0:T(8,128)S(1)} %copy-done) | data formatting | bytes 8388608
  169.3 0.0 copy-done.1
  169.4 0.7 copy.19
Async XLA Ops:
  162.6 4.8 %copy-start = (f32[128,8192]{1,0:T(8,128)S(1)}, f32[128,8192]{1,0:T(8,128)}, u32[]{:S(2)}) copy-start(f32[128,8192]{1,0:T(8,128)} %get-tuple-element.21) | copy-start | bytes 12582916
  167.3 2.0 %copy-start.1 = (f32[4,8192]{1,0:T(4,128)S(1)}, f32[4,8192]{1,0:T(4,128)}, u32[]{:S(2)}) copy-start(f32[4,8192]{1,0:T(4,128)} %get-tuple-element.22) | copy-start | bytes 393220
